TPU v7x, 128 devices: a whole 4x4x4 slice. The times are simulated.
128 devices in a mesh: gx: 8 (over x_lo, z), gy: 4 (over y), gz: 4 (over x_hi, core).
Axes of the slice: x: 4 (x_hi: 2, x_lo: 2; x = x_hi * 2 + x_lo), y: 4, z: 4, core: 2. Of those that a mesh axis runs over, the one named last changes fastest.
Arguments:
- inputs: bfloat16 [2560, 8192], P(('gx', 'gz'), 'gy'), may hold values from -6 to 6
- out_grad: bfloat16 [2560, 8192], P(('gx', 'gz'), 'gy'), may hold values from -6 to 6
- gate_weight: bfloat16 [8192, 16384], P('gy', ('gx', 'gz')), may hold values from -0.0625 to 0.0625
- up_weight: bfloat16 [8192, 16384], P('gy', ('gx', 'gz')), may hold values from -0.0625 to 0.0625
- down_weight: bfloat16 [16384, 8192], P(('gx', 'gz'), 'gy'), may hold values from -0.046875 to 0.046875
Outputs:
- in_grad: bfloat16 [2560, 8192], P(('gx', 'gz'), 'gy')
All inputs are finite; a program needn't handle non-finite values.
Results may differ from a plain program's by a relative error of at most 0.0049.
Values may be sent and summed in bfloat16 or wider, within the bound.
A program may use at most 128 MiB of HBM per device.

v0:
```python
import jax
import jax.numpy as jnp
from jax import lax
from jax.experimental import pallas as pl
from jax.experimental.pallas import tpu as pltpu
from jax.sharding import PartitionSpec as P

MESH = pl.DeviceIdType.MESH
F32 = jnp.float32
BF16 = jnp.bfloat16

ROWS = 80
WIDTH = 2048
HALF = WIDTH // 2
OWN = 512
Q = 256
CUT = 3 * Q // 2

GROUPS = (
    ((0, 0, 0, 80),),
    ((0, 1, 0, 48), (0, 3, 0, 48)),
    ((1, 0, 0, 48), (3, 0, 0, 48)),
    ((1, 1, 0, 80), (3, 3, 0, 80)),
    ((1, 3, 0, 80), (3, 1, 0, 80)),
    ((2, 2, 0, 80), (1, 2, 0, 80), (2, 1, 0, 48)),
    ((3, 2, 0, 80), (2, 3, 0, 80), (2, 1, 48, 32)),
    ((0, 2, 0, 80), (2, 0, 0, 80)),
    ((1, 0, 48, 32), (3, 0, 48, 32), (0, 1, 48, 32), (0, 3, 48, 32)),
)
EARLY = 48
SIZES = tuple(sum(rows for *_, rows in group) for group in GROUPS)
STARTS = tuple(sum(SIZES[:g]) for g in range(len(SIZES)))
TOP = max(SIZES)
ALL = sum(SIZES)


def contract_last(left, right):
    return lax.dot_general(
        left, right, (((1,), (1,)), ((), ())), preferred_element_type=F32
    )


class Copies:
    def __init__(self, send_sems, recv_sems):
        self.send_sems, self.recv_sems = send_sems, recv_sems
        self.made, self.sent, self.landed = {}, {}, set()
        self.keys, self.user = {}, {}

    def send(self, name, src, dst, device):
        k = len(self.made) % SENDS
        for old in [old for old, at in self.sent.items() if at == k]:
            self.free(old)
        key = name[:3] + str(int(name[3:]) % 3) if name[:2] in OVER_Y else name
        r = self.keys.setdefault(key, len(self.keys))
        assert self.user.get(key, name) == name or self.user[key] in self.landed
        self.user[key] = name
        copy = pltpu.make_async_remote_copy(
            src_ref=src,
            dst_ref=dst,
            send_sem=self.send_sems.at[k],
            recv_sem=self.recv_sems.at[r],
            device_id=device,
            device_id_type=MESH,
        )
        self.made[name] = copy
        self.sent[name] = k
        copy.start()

    def need(self, *names):
        for name in names:
            if name not in self.landed:
                self.landed.add(name)
                self.made[name].wait_recv()

    def free(self, *names):
        for name in names:
            if name in self.sent:
                del self.sent[name]
                self.made[name].wait_send()

    def finish(self):
        assert len(self.keys) == RECVS
        self.need(*self.made)
        self.free(*list(self.sent))


OVER_Y = ("ra", "rb", "ga", "gf")
SENDS = 40
RECVS = 104


def kernel(
    x_hbm, g_hbm, wg_hbm, wu_hbm, wd_hbm, out_ref,
    A, B, Wgu, Wd, S, O, ra, rb, H, sa, sb, xsa, xsb, xa, xb, xd, zs, zt, zr,
    send_sems, recv_sems, local_sems, weight_sends, weight_sems,
):
    gx, y, gz = lax.axis_index("gx"), lax.axis_index("gy"), lax.axis_index("gz")
    x = lax.div(gz, 2) * 2 + lax.div(gx, 4)
    z = lax.rem(gx, 4)
    core = lax.rem(gz, 2)

    def device(dx=0, dy=0, dz=0):
        nx, ny, nz = (lax.rem(p + d + 4, 4) for p, d in ((x, dx), (y, dy), (z, dz)))
        return {
            "gx": lax.rem(nx, 2) * 4 + nz,
            "gy": ny,
            "gz": lax.div(nx, 2) * 2 + core,
        }

    partner = {"gx": gx, "gy": y, "gz": gz + 1 - 2 * core}
    xp, xm = device(dx=1), device(dx=-1)
    yp, ym = device(dy=1), device(dy=-1)
    zp, zm = device(dz=1), device(dz=-1)

    barrier = pltpu.get_barrier_semaphore()
    peers = (partner, xp, xm, yp, ym, zp, zm)
    own_tokens = [
        pltpu.make_async_copy(src, ref.at[0, 0], local_sems.at[k])
        for k, (src, ref) in enumerate(((x_hbm, A), (g_hbm, B)))
    ]
    for copy in own_tokens:
        copy.start()
    for peer in peers:
        pl.semaphore_signal(barrier, inc=1, device_id=peer, device_id_type=MESH)
    pl.semaphore_wait(barrier, len(peers))

    c = Copies(send_sems, recv_sems)
    L, R = pl.ds(0, HALF), pl.ds(HALF, HALF)

    near = lax.rem(y + 2, 4)
    mine = 1 - jnp.abs(lax.div(near, 2) - core)
    lead = mine * lax.rem(near, 2)
    locals_ = []

    def local(src, dst, sem):
        copy = pltpu.make_async_copy(src, dst, sem)
        copy.start()
        return copy

    def pieces(q, j):
        wide, narrow = pl.multiple_of(q * 2 * Q, 2 * Q), pl.multiple_of(q * Q, Q)
        part = pl.ds(pl.multiple_of(j * Q, Q), Q)
        return (
            (wg_hbm.at[:, part], Wgu.at[:, pl.ds(wide, Q)]),
            (wu_hbm.at[:, part], Wgu.at[:, pl.ds(wide + Q, Q)]),
            (wd_hbm.at[part], Wd.at[pl.ds(narrow, Q)]),
        )

    own = [(2 * core + j, j) for j in (lead, 1 - lead)]
    for n, (q, j) in enumerate(own):
        for k, (src, dst) in enumerate(pieces(q, j)):
            copy = pltpu.make_async_remote_copy(
                src_ref=src,
                dst_ref=dst,
                send_sem=weight_sends.at[3 * n + k],
                recv_sem=weight_sems.at[3 * q + k],
                device_id=partner,
                device_id_type=MESH,
            )
            copy.start()
            locals_.append(copy)

    def own_over_x(name, hbm, ref, rows):
        c.send(name.replace("@", "+"), hbm.at[rows], ref.at[0, 3, rows], xp)
        c.send(name.replace("@", "-"), hbm.at[rows], ref.at[0, 1, rows], xm)

    def own_over_z(name, hbm, ref, rows):
        c.send(name.replace("@", "+"), hbm.at[rows], ref.at[3, 0, rows], zp)
        c.send(name.replace("@", "-"), hbm.at[rows], ref.at[1, 0, rows], zm)

    ahead, behind = pl.ds(0, EARLY), pl.ds(EARLY, ROWS - EARLY)
    own_over_x("Ax@", x_hbm, A, ahead)
    own_over_z("Bz@", g_hbm, B, ahead)
    own_over_x("Bx@0", g_hbm, B, ahead)
    own_over_z("Az@0", x_hbm, A, ahead)
    own_over_x("Ax@b", x_hbm, A, behind)
    own_over_z("Bz@b", g_hbm, B, behind)

    def need_weights(q):
        for k, (src, dst) in enumerate(pieces(q, 0)):
            pltpu.make_async_copy(src, dst, weight_sems.at[3 * q + k]).wait()

    def a_over_z(dx):
        c.send(f"Az+{dx}", A.at[0, dx], A.at[3, dx], zp)
        c.send(f"Az-{dx}", A.at[0, dx], A.at[1, dx], zm)

    def a_over_z_far(dx):
        c.need(f"Az+{dx}", f"Az-{dx}")
        if dx == 0:
            c.need("Az+0b", "Az-0b")
        c.send(f"Azf+{dx}", A.at[3, dx, :, L], A.at[2, dx, :, L], zp)
        c.send(f"Azf-{dx}", A.at[1, dx, :, R], A.at[2, dx, :, R], zm)

    def b_over_x(dz):
        c.send(f"Bx+{dz}", B.at[dz, 0], B.at[dz, 3], xp)
        c.send(f"Bx-{dz}", B.at[dz, 0], B.at[dz, 1], xm)

    def b_over_x_far(dz):
        c.need(f"Bx+{dz}", f"Bx-{dz}")
        if dz == 0:
            c.need("Bx+0b", "Bx-0b")
        c.send(f"Bxf+{dz}", B.at[dz, 3, :, L], B.at[dz, 2, :, L], xp)
        c.send(f"Bxf-{dz}", B.at[dz, 1, :, R], B.at[dz, 2, :, R], xm)

    def relay_1():
        c.need("Ax+", "Ax-", "Ax+b", "Ax-b")
        c.send("Az-1", A.at[0, 1], A.at[1, 1], zm)
        c.send("Az+3", A.at[0, 3], A.at[3, 3], zp)
        c.need("Bz+", "Bz-", "Bz+b", "Bz-b")
        c.send("Bx-1", B.at[1, 0], B.at[1, 1], xm)
        c.send("Bx+3", B.at[3, 0], B.at[3, 3], xp)
        c.send("Axf+", A.at[0, 3, :, L], A.at[0, 2, :, L], xp)
        c.send("Axf-", A.at[0, 1, :, R], A.at[0, 2, :, R], xm)
        c.send("Bzf+", B.at[3, 0, :, L], B.at[2, 0, :, L], zp)
        c.send("Bzf-", B.at[1, 0, :, R], B.at[2, 0, :, R], zm)
        c.send("Az+1", A.at[0, 1], A.at[3, 1], zp)
        c.send("Az-3", A.at[0, 3], A.at[1, 3], zm)
        c.send("Bx+1", B.at[1, 0], B.at[1, 3], xp)
        c.send("Bx-3", B.at[3, 0], B.at[3, 1], xm)

    def relay_2():
        c.need("Bzf+", "Bzf-")
        b_over_x(2)
        c.need("Axf+", "Axf-")
        a_over_z(2)

    def relay_3():
        b_over_x_far(1)
        a_over_z_far(1)

    def relay_4():
        a_over_z_far(2)
        b_over_x_far(2)
        a_over_z_far(3)
        b_over_x_far(3)
        own_over_z("Az@0b", x_hbm, A, behind)

    def relay_5():
        own_over_x("Bx@0b", g_hbm, B, behind)

    def relay_6():
        a_over_z_far(0)
        b_over_x_far(0)

    relays = {5: relay_5, 6: relay_6}

    def need_tokens(g):
        for dz, dx, first, _ in GROUPS[g]:
            late = first >= EARLY
            if dz == 0:
                c.need(*{0: (), 1: ("Ax-", "Bx-0"), 2: ("Axf+", "Axf-", "Bxf+0", "Bxf-0"), 3: ("Ax+", "Bx+0")}[dx])
                if late:
                    c.need(*{0: (), 1: ("Ax-b", "Bx-0b"), 2: (), 3: ("Ax+b", "Bx+0b")}[dx])
                continue
            c.need(*{1: (f"Az-{dx}",), 2: (f"Azf+{dx}", f"Azf-{dx}"), 3: (f"Az+{dx}",)}[dz])
            if dx == 0:
                c.need(*{1: ("Bz-",), 2: ("Bzf+", "Bzf-"), 3: ("Bz+",)}[dz])
                if late:
                    c.need(*{1: ("Az-0b", "Bz-b"), 2: (), 3: ("Az+0b", "Bz+b")}[dz])
            else:
                c.need(*{1: (f"Bx-{dz}",), 2: (f"Bxf+{dz}", f"Bxf-{dz}"), 3: (f"Bx+{dz}",)}[dx])

    def rows_of(ref, g):
        parts = [ref[dz, dx, first : first + rows] for dz, dx, first, rows in GROUPS[g]]
        return parts[0] if len(parts) == 1 else jnp.concatenate(parts, axis=0)

    def quarter(k):
        return lax.rem(y + k, 4)

    def forward(g, start=0, stop=4):
        m = SIZES[g]
        need_tokens(g)

        @pl.loop(start, stop)
        def _(k):
            q = lax.rem(y + 2 + k, 4)
            if g == 0:
                need_weights(q)
            w = Wgu[:, pl.ds(pl.multiple_of(q * 2 * Q, 2 * Q), 2 * Q)]
            S[g % 2, k, 0:m, 0 : 2 * Q] = jnp.dot(rows_of(A, g), w, preferred_element_type=F32)
            d = Wd[pl.ds(pl.multiple_of(q * Q, Q), Q), :]
            S[g % 2, k, 0:m, 2 * Q : 3 * Q] = contract_last(rows_of(B, g), d)

    def reduce_far(g):
        s, m = g % 2, SIZES[g]
        at = pl.ds(STARTS[g], m)
        if g >= 2:
            c.free(f"ra+{g - 2}", f"ra-{g - 2}")
        sa[s, 0:m] = S[s, 0, 0:m].astype(BF16)
        c.send(f"ra+{g}", sa.at[s, pl.ds(0, m), pl.ds(0, CUT)], ra.at[0, at], yp)
        c.send(f"ra-{g}", sa.at[s, pl.ds(0, m), pl.ds(CUT, CUT)], ra.at[1, at], ym)

    def reduce_near(g):
        s, m = g % 2, SIZES[g]
        at = slice(STARTS[g], STARTS[g] + m)
        if g >= 2:
            c.free(f"rb+{g - 2}", f"rb-{g - 2}")
        c.need(f"ra+{g}", f"ra-{g}")
        sb[s, 0, 0:m, 0:CUT] = (S[s, 3, 0:m, 0:CUT] + ra[0, at].astype(F32)).astype(BF16)
        sb[s, 0, 0:m, CUT:] = S[s, 3, 0:m, CUT:].astype(BF16)
        c.send(f"rb+{g}", sb.at[s, 0, pl.ds(0, m)], rb.at[0, pl.ds(STARTS[g], m)], yp)
        sb[s, 1, 0:m, 0:CUT] = S[s, 1, 0:m, 0:CUT].astype(BF16)
        sb[s, 1, 0:m, CUT:] = (S[s, 1, 0:m, CUT:] + ra[1, at].astype(F32)).astype(BF16)
        c.send(f"rb-{g}", sb.at[s, 1, pl.ds(0, m)], rb.at[1, pl.ds(STARTS[g], m)], ym)

    last = len(GROUPS) - 1

    def grads(g):
        s, m = g % 2, SIZES[g]
        rows = pl.ds(STARTS[g], m)
        c.need(f"rb+{g}", f"rb-{g}")

        def total(at):
            cols = pl.ds(at, Q)
            return S[s, 2, 0:m, cols] + rb[0, rows, cols].astype(F32) + rb[1, rows, cols].astype(F32)

        gate, upper, hidden_grad = total(0), total(Q), total(2 * Q)
        logistic = 1.0 / (1.0 + jnp.exp(-gate))
        scaled = hidden_grad * logistic
        at = pl.multiple_of(y * (2 * Q), 2 * Q)
        H[rows, pl.ds(at, Q)] = (scaled * upper * (1.0 + gate * (1.0 - logistic))).astype(BF16)
        H[rows, pl.ds(at + Q, Q)] = (scaled * gate).astype(BF16)
        own = H.at[rows, pl.ds(at, 2 * Q)]
        c.send(f"ga+{g}", own, own, yp)
        c.send(f"ga-{g}", own, own, ym)

    def spread(g):
        rows = pl.ds(STARTS[g], SIZES[g])
        c.need(f"ga+{g}", f"ga-{g}")
        at = pl.multiple_of(quarter(3) * (2 * Q), 2 * Q)
        part = H.at[rows, pl.ds(at, Q)]
        c.send(f"gf+{g}", part, part, yp)
        at = pl.multiple_of(quarter(1) * (2 * Q), 2 * Q)
        part = H.at[rows, pl.ds(at + Q, Q)]
        c.send(f"gf-{g}", part, part, ym)

    def product(g, start=0, steps=4):
        rows = slice(STARTS[g], STARTS[g] + SIZES[g])
        c.need(f"gf+{g}", f"gf-{g}")

        @pl.loop(start, start + steps)
        def _(n):
            cols = pl.ds(pl.multiple_of(n * 512, 512), 512)
            o = contract_last(H[rows], Wgu[cols, :])
            done = 0
            for dz, dx, first, count in GROUPS[g]:
                O[dz, dx, first : first + count, cols] = o[done : done + count]
                done += count

    def backward(g):
        product(g)
        run(after.get(g, ()))

    def out_down(r):
        xsa[r] = O[r, 2].astype(BF16)
        c.send(f"d{r}", xsa.at[r], xd.at[r], {1: zp, 3: zm}[r])

    def out_far(r):
        total = O[r, 2]
        if r == 0:
            c.need("d1", "d3")
            total = total + xd[1].astype(F32) + xd[3].astype(F32)
        xsa[r] = total.astype(BF16)
        c.send(f"xa+{r}", xsa.at[r, :, L], xa.at[r // 2, 0], xp)
        c.send(f"xa-{r}", xsa.at[r, :, R], xa.at[r // 2, 1], xm)

    def out_pass(r):
        c.need(f"xa+{r}", f"xa-{r}")
        c.send(f"xd+{r}", xa.at[r // 2, 0], xd.at[r, :, L], xp)
        c.send(f"xd-{r}", xa.at[r // 2, 1], xd.at[r, :, R], xm)

    def out_near(r, dx, rows=(0, ROWS), halves=(0, 1)):
        k, sign, device = {1: (0, "+", xp), 3: (1, "-", xm)}[dx]
        at, to = slice(*rows), pl.ds(rows[0], rows[1] - rows[0])
        cols = pl.ds(halves[0] * HALF, len(halves) * HALF)
        xsb[r, k, at, cols] = O[r, dx, at, cols].astype(BF16)
        c.send(f"xb{sign}{r}_{rows[0]}_{halves[0]}", xsb.at[r, k, to, cols], xb.at[r, k, to, cols], device)

    def over_x(r, at, cols):
        near = O[r, 0, at, cols] + xb[r, 0, at, cols].astype(F32) + xb[r, 1, at, cols].astype(F32)
        return near + xd[r, at, cols].astype(F32) if r in (0, 2) else near

    def out_sum(r, rows=(0, ROWS), halves=(0, 1)):
        c.need(f"xb+{r}_0_0", f"xb-{r}_0_0")
        if r == 2:
            c.need("xd+2", "xd-2")
        at, to = slice(*rows), pl.ds(rows[0], rows[1] - rows[0])
        cols = pl.ds(halves[0] * HALF, len(halves) * HALF)
        zs[r - 1, at, cols] = over_x(r, at, cols).astype(BF16)
        if r == 2:
            c.send("z2+", zs.at[1, :, L], zt.at[0], zp)
            c.send("z2-", zs.at[1, :, R], zt.at[1], zm)
        else:
            name = f"z{r}_{rows[0]}_{halves[0]}"
            c.send(name, zs.at[r - 1, to, cols], zr.at[r - 1, to, cols], {1: zp, 3: zm}[r])

    def out_sum_far():
        c.need("z2+", "z2-")
        c.send("z2f+", zt.at[0], zr.at[1, :, L], zp)
        c.send("z2f-", zt.at[1], zr.at[1, :, R], zm)

    def out_final(first, rows):
        at = slice(first, first + rows)
        total = over_x(0, at, slice(0, WIDTH))
        for k in range(3):
            total += zr[k, at].astype(F32)
        out_ref[at] = total.astype(BF16)

    after = {
        1: ((out_near, 0, 1, (0, EARLY)), (out_near, 0, 3, (0, EARLY))),
        3: ((out_near, 1, 1), (out_near, 3, 3)),
        4: ((out_near, 1, 3), (out_near, 3, 1)),
        5: ((out_far, 2), (out_down, 1), (out_sum, 1, (0, EARLY)), (out_sum, 3, (0, EARLY))),
        6: ((out_down, 3), (out_near, 2, 1), (out_near, 2, 3)),
        7: ((out_far, 0),),
    }

    def run(events):
        for event, *args in events:
            event(*args)

    for n, (q, j) in enumerate(own):
        for k, (src, dst) in enumerate(pieces(q, j)):
            local(src, dst, weight_sems.at[3 * q + k])
    for copy in own_tokens:
        copy.wait()
    forward(0, 0, 1)
    reduce_far(0)
    forward(0, 1, 4)
    reduce_near(0)
    forward(1)
    reduce_far(1)
    relay_1()
    grads(0)
    forward(2)
    reduce_far(2)
    reduce_near(1)
    spread(0)
    reduce_near(2)
    grads(1)
    forward(3)
    reduce_far(3)
    relay_2()
    backward(0)
    spread(1)
    relay_3()
    for t in range(3, last):
        if t > 3:
            reduce_far(t)
        if t == 4:
            relay_4()
        grads(t - 1)
        backward(t - 2)
        reduce_near(t)
        if t + 1 in relays:
            relays[t + 1]()
        forward(t + 1)
        spread(t - 1)
    reduce_far(last)
    grads(last - 1)
    out_pass(2)
    backward(last - 2)
    reduce_near(last)
    spread(last - 1)
    grads(last)
    backward(last - 1)
    spread(last)
    out_sum(2)
    for h in (0, 1):
        product(last, 2 * h, 2)
        out_near(0, 1, (EARLY, ROWS), (h,))
        out_near(0, 3, (EARLY, ROWS), (h,))
        out_sum(1, (EARLY, ROWS), (h,))
        out_sum(3, (EARLY, ROWS), (h,))
        if h == 0:
            out_pass(0)
    out_sum_far()
    for copy in locals_:
        copy.wait_send()
    c.finish()
    out_final(0, ROWS // 2)
    out_final(ROWS // 2, ROWS // 2)


def shards(inputs, out_grad, gate_weight, up_weight, down_weight):
    return pl.pallas_call(
        kernel,
        out_shape=pltpu.VMEM((ROWS, WIDTH), BF16),
        in_specs=[pl.BlockSpec(memory_space=pl.ANY)] * 5,
        out_specs=pl.BlockSpec(memory_space=pltpu.VMEM),
        scratch_shapes=[
            pltpu.VMEM((4, 4, ROWS, WIDTH), BF16),
            pltpu.VMEM((4, 4, ROWS, WIDTH), BF16),
            pltpu.VMEM((WIDTH, 8 * Q), BF16),
            pltpu.VMEM((4 * Q, WIDTH), BF16),
            pltpu.VMEM((2, 4, TOP, 3 * Q), F32),
            pltpu.VMEM((4, 4, ROWS, WIDTH), F32),
            pltpu.VMEM((2, ALL, CUT), BF16),
            pltpu.VMEM((2, ALL, 3 * Q), BF16),
            pltpu.VMEM((ALL, 8 * Q), BF16),
            pltpu.VMEM((2, TOP, 3 * Q), BF16),
            pltpu.VMEM((2, 2, TOP, 3 * Q), BF16),
            pltpu.VMEM((4, ROWS, WIDTH), BF16),
            pltpu.VMEM((4, 2, ROWS, WIDTH), BF16),
            pltpu.VMEM((2, 2, ROWS, HALF), BF16),
            pltpu.VMEM((4, 2, ROWS, WIDTH), BF16),
            pltpu.VMEM((4, ROWS, WIDTH), BF16),
            pltpu.VMEM((3, ROWS, WIDTH), BF16),
            pltpu.VMEM((2, ROWS, HALF), BF16),
            pltpu.VMEM((3, ROWS, WIDTH), BF16),
            pltpu.SemaphoreType.DMA((SENDS,)),
            pltpu.SemaphoreType.DMA((RECVS,)),
            pltpu.SemaphoreType.DMA((2,)),
            pltpu.SemaphoreType.DMA((6,)),
            pltpu.SemaphoreType.DMA((12,)),
        ],
        compiler_params=pltpu.CompilerParams(
            collective_id=0, has_side_effects=True, vmem_limit_bytes=65_000_000
        ),
        name="swiglu_back",
    )(inputs, out_grad, gate_weight, up_weight, down_weight)


def solution(mesh):
    return jax.shard_map(
        shards,
        mesh=mesh,
        in_specs=(
            P(("gx", "gz"), "gy"),
            P(("gx", "gz"), "gy"),
            P("gy", ("gx", "gz")),
            P("gy", ("gx", "gz")),
            P(("gx", "gz"), "gy"),
        ),
        out_specs=P(("gx", "gz"), "gy"),
        check_vma=False,
    )
```

profile of v0, /device:TPU:0, one launch (start us, length us, event | category | flops | bytes accessed | tf_op | source)
XLA Modules:
  0.0 145.9 jit_solution(10158225652482344876)
XLA Ops:
  0.0 145.2 %swiglu_back.1 = bf16[80,2048]{1,0:T(8,128)(2,1)S(1)} custom-call(bf16[80,2048]{1,0:T(8,128)(2,1)} %x_hbm.1, bf16[80,2048]{1,0:T(8,128)(2,1)} %g_hbm.1, bf16[2048,512]{1,0:T(8,128)(2,1)} %wg_hbm.1, bf16[2048,512]{1,0:T(8,128)(2,1)} %wu_hbm.1, bf16[512,2048]{1,0:T(8,128)(2,1)} %wd_hbm.1), custom_call_target="tpu_custom_call" | custom-call | tf_op jit(solution)/shard_map/swiglu_back/pallas_call | solution.py:486
  145.2 0.7 copy.7
where the time goes:
time: 146 us
  Pallas kernels  145 us (99%)
    pallas_call x1, Pallas kernels, shards(): pl.pallas_call(kernel, out_shape=pltpu.VMEM((ROWS, WIDTH), BF16), in_spec...  145 us

commit v1 on v0

--- a/solution.py
+++ b/solution.py
@@ -44,16 +44,17 @@
     def __init__(self, send_sems, recv_sems):
         self.send_sems, self.recv_sems = send_sems, recv_sems
         self.made, self.sent, self.landed = {}, {}, set()
-        self.keys, self.user = {}, {}
-
-    def send(self, name, src, dst, device):
+        self.keys, self.user, self.pairs = {}, {}, {}
+
+    def send(self, name, src, dst, device, both=None):
         k = len(self.made) % SENDS
         for old in [old for old, at in self.sent.items() if at == k]:
             self.free(old)
-        key = name[:3] + str(int(name[3:]) % 3) if name[:2] in OVER_Y else name
+        base = name if both is None else name.replace("+", "").replace("-", "")
+        key = base[:2] + str(int(base[2:]) % 3) if base[:2] in OVER_Y else base
         r = self.keys.setdefault(key, len(self.keys))
-        assert self.user.get(key, name) == name or self.user[key] in self.landed
-        self.user[key] = name
+        assert self.user.get(key, base) == base or self.user[key] in self.landed
+        self.user[key] = base
         copy = pltpu.make_async_remote_copy(
             src_ref=src,
             dst_ref=dst,
@@ -64,13 +65,19 @@
         )
         self.made[name] = copy
         self.sent[name] = k
+        if both is not None:
+            self.pairs[name] = base, (both, both, self.recv_sems.at[r])
         copy.start()
 
     def need(self, *names):
         for name in names:
-            if name not in self.landed:
-                self.landed.add(name)
-                self.made[name].wait_recv()
+            base, pair = self.pairs.get(name, (name, None))
+            if base not in self.landed:
+                self.landed.add(base)
+                if pair is None:
+                    self.made[name].wait_recv()
+                else:
+                    pltpu.make_async_copy(*pair).wait()
 
     def free(self, *names):
         for name in names:
@@ -85,8 +92,8 @@
 
 
 OVER_Y = ("ra", "rb", "ga", "gf")
-SENDS = 40
-RECVS = 104
+SENDS = 28
+RECVS = 76
 
 
 def kernel(
@@ -188,8 +195,8 @@
         c.need(f"Az+{dx}", f"Az-{dx}")
         if dx == 0:
             c.need("Az+0b", "Az-0b")
-        c.send(f"Azf+{dx}", A.at[3, dx, :, L], A.at[2, dx, :, L], zp)
-        c.send(f"Azf-{dx}", A.at[1, dx, :, R], A.at[2, dx, :, R], zm)
+        c.send(f"Azf+{dx}", A.at[3, dx, :, L], A.at[2, dx, :, L], zp, A.at[2, dx])
+        c.send(f"Azf-{dx}", A.at[1, dx, :, R], A.at[2, dx, :, R], zm, A.at[2, dx])
 
     def b_over_x(dz):
         c.send(f"Bx+{dz}", B.at[dz, 0], B.at[dz, 3], xp)
@@ -199,8 +206,8 @@
         c.need(f"Bx+{dz}", f"Bx-{dz}")
         if dz == 0:
             c.need("Bx+0b", "Bx-0b")
-        c.send(f"Bxf+{dz}", B.at[dz, 3, :, L], B.at[dz, 2, :, L], xp)
-        c.send(f"Bxf-{dz}", B.at[dz, 1, :, R], B.at[dz, 2, :, R], xm)
+        c.send(f"Bxf+{dz}", B.at[dz, 3, :, L], B.at[dz, 2, :, L], xp, B.at[dz, 2])
+        c.send(f"Bxf-{dz}", B.at[dz, 1, :, R], B.at[dz, 2, :, R], xm, B.at[dz, 2])
 
     def relay_1():
         c.need("Ax+", "Ax-", "Ax+b", "Ax-b")
@@ -209,10 +216,10 @@
         c.need("Bz+", "Bz-", "Bz+b", "Bz-b")
         c.send("Bx-1", B.at[1, 0], B.at[1, 1], xm)
         c.send("Bx+3", B.at[3, 0], B.at[3, 3], xp)
-        c.send("Axf+", A.at[0, 3, :, L], A.at[0, 2, :, L], xp)
-        c.send("Axf-", A.at[0, 1, :, R], A.at[0, 2, :, R], xm)
-        c.send("Bzf+", B.at[3, 0, :, L], B.at[2, 0, :, L], zp)
-        c.send("Bzf-", B.at[1, 0, :, R], B.at[2, 0, :, R], zm)
+        c.send("Axf+", A.at[0, 3, :, L], A.at[0, 2, :, L], xp, A.at[0, 2])
+        c.send("Axf-", A.at[0, 1, :, R], A.at[0, 2, :, R], xm, A.at[0, 2])
+        c.send("Bzf+", B.at[3, 0, :, L], B.at[2, 0, :, L], zp, B.at[2, 0])
+        c.send("Bzf-", B.at[1, 0, :, R], B.at[2, 0, :, R], zm, B.at[2, 0])
         c.send("Az+1", A.at[0, 1], A.at[3, 1], zp)
         c.send("Az-3", A.at[0, 3], A.at[1, 3], zm)
         c.send("Bx+1", B.at[1, 0], B.at[1, 3], xp)
@@ -287,21 +294,21 @@
         if g >= 2:
             c.free(f"ra+{g - 2}", f"ra-{g - 2}")
         sa[s, 0:m] = S[s, 0, 0:m].astype(BF16)
-        c.send(f"ra+{g}", sa.at[s, pl.ds(0, m), pl.ds(0, CUT)], ra.at[0, at], yp)
-        c.send(f"ra-{g}", sa.at[s, pl.ds(0, m), pl.ds(CUT, CUT)], ra.at[1, at], ym)
+        c.send(f"ra+{g}", sa.at[s, pl.ds(0, m), pl.ds(0, CUT)], ra.at[0, at], yp, ra.at[:, at])
+        c.send(f"ra-{g}", sa.at[s, pl.ds(0, m), pl.ds(CUT, CUT)], ra.at[1, at], ym, ra.at[:, at])
 
     def reduce_near(g):
         s, m = g % 2, SIZES[g]
-        at = slice(STARTS[g], STARTS[g] + m)
+        at, rows = slice(STARTS[g], STARTS[g] + m), pl.ds(STARTS[g], m)
         if g >= 2:
             c.free(f"rb+{g - 2}", f"rb-{g - 2}")
         c.need(f"ra+{g}", f"ra-{g}")
         sb[s, 0, 0:m, 0:CUT] = (S[s, 3, 0:m, 0:CUT] + ra[0, at].astype(F32)).astype(BF16)
         sb[s, 0, 0:m, CUT:] = S[s, 3, 0:m, CUT:].astype(BF16)
-        c.send(f"rb+{g}", sb.at[s, 0, pl.ds(0, m)], rb.at[0, pl.ds(STARTS[g], m)], yp)
+        c.send(f"rb+{g}", sb.at[s, 0, pl.ds(0, m)], rb.at[0, rows], yp, rb.at[:, rows])
         sb[s, 1, 0:m, 0:CUT] = S[s, 1, 0:m, 0:CUT].astype(BF16)
         sb[s, 1, 0:m, CUT:] = (S[s, 1, 0:m, CUT:] + ra[1, at].astype(F32)).astype(BF16)
-        c.send(f"rb-{g}", sb.at[s, 1, pl.ds(0, m)], rb.at[1, pl.ds(STARTS[g], m)], ym)
+        c.send(f"rb-{g}", sb.at[s, 1, pl.ds(0, m)], rb.at[1, rows], ym, rb.at[:, rows])
 
     last = len(GROUPS) - 1
 
@@ -321,18 +328,18 @@
         H[rows, pl.ds(at, Q)] = (scaled * upper * (1.0 + gate * (1.0 - logistic))).astype(BF16)
         H[rows, pl.ds(at + Q, Q)] = (scaled * gate).astype(BF16)
         own = H.at[rows, pl.ds(at, 2 * Q)]
-        c.send(f"ga+{g}", own, own, yp)
-        c.send(f"ga-{g}", own, own, ym)
+        c.send(f"ga+{g}", own, own, yp, H.at[rows, pl.ds(0, 4 * Q)])
+        c.send(f"ga-{g}", own, own, ym, H.at[rows, pl.ds(0, 4 * Q)])
 
     def spread(g):
         rows = pl.ds(STARTS[g], SIZES[g])
         c.need(f"ga+{g}", f"ga-{g}")
         at = pl.multiple_of(quarter(3) * (2 * Q), 2 * Q)
         part = H.at[rows, pl.ds(at, Q)]
-        c.send(f"gf+{g}", part, part, yp)
+        c.send(f"gf+{g}", part, part, yp, H.at[rows, pl.ds(0, 2 * Q)])
         at = pl.multiple_of(quarter(1) * (2 * Q), 2 * Q)
         part = H.at[rows, pl.ds(at + Q, Q)]
-        c.send(f"gf-{g}", part, part, ym)
+        c.send(f"gf-{g}", part, part, ym, H.at[rows, pl.ds(0, 2 * Q)])
 
     def product(g, start=0, steps=4):
         rows = slice(STARTS[g], STARTS[g] + SIZES[g])
@@ -361,13 +368,13 @@
             c.need("d1", "d3")
             total = total + xd[1].astype(F32) + xd[3].astype(F32)
         xsa[r] = total.astype(BF16)
-        c.send(f"xa+{r}", xsa.at[r, :, L], xa.at[r // 2, 0], xp)
-        c.send(f"xa-{r}", xsa.at[r, :, R], xa.at[r // 2, 1], xm)
+        c.send(f"xa+{r}", xsa.at[r, :, L], xa.at[r // 2, 0], xp, xa.at[r // 2])
+        c.send(f"xa-{r}", xsa.at[r, :, R], xa.at[r // 2, 1], xm, xa.at[r // 2])
 
     def out_pass(r):
         c.need(f"xa+{r}", f"xa-{r}")
-        c.send(f"xd+{r}", xa.at[r // 2, 0], xd.at[r, :, L], xp)
-        c.send(f"xd-{r}", xa.at[r // 2, 1], xd.at[r, :, R], xm)
+        c.send(f"xd+{r}", xa.at[r // 2, 0], xd.at[r, :, L], xp, xd.at[r])
+        c.send(f"xd-{r}", xa.at[r // 2, 1], xd.at[r, :, R], xm, xd.at[r])
 
     def out_near(r, dx, rows=(0, ROWS), halves=(0, 1)):
         k, sign, device = {1: (0, "+", xp), 3: (1, "-", xm)}[dx]
@@ -388,16 +395,16 @@
         cols = pl.ds(halves[0] * HALF, len(halves) * HALF)
         zs[r - 1, at, cols] = over_x(r, at, cols).astype(BF16)
         if r == 2:
-            c.send("z2+", zs.at[1, :, L], zt.at[0], zp)
-            c.send("z2-", zs.at[1, :, R], zt.at[1], zm)
+            c.send("z2+", zs.at[1, :, L], zt.at[0], zp, zt)
+            c.send("z2-", zs.at[1, :, R], zt.at[1], zm, zt)
         else:
             name = f"z{r}_{rows[0]}_{halves[0]}"
             c.send(name, zs.at[r - 1, to, cols], zr.at[r - 1, to, cols], {1: zp, 3: zm}[r])
 
     def out_sum_far():
         c.need("z2+", "z2-")
-        c.send("z2f+", zt.at[0], zr.at[1, :, L], zp)
-        c.send("z2f-", zt.at[1], zr.at[1, :, R], zm)
+        c.send("z2f+", zt.at[0], zr.at[1, :, L], zp, zr.at[1])
+        c.send("z2f-", zt.at[1], zr.at[1, :, R], zm, zr.at[1])
 
     def out_final(first, rows):
         at = slice(first, first + rows)
@@ -466,15 +473,20 @@
     backward(last - 1)
     spread(last)
     out_sum(2)
-    for h in (0, 1):
-        product(last, 2 * h, 2)
+
+    def out_last(h):
         out_near(0, 1, (EARLY, ROWS), (h,))
         out_near(0, 3, (EARLY, ROWS), (h,))
         out_sum(1, (EARLY, ROWS), (h,))
         out_sum(3, (EARLY, ROWS), (h,))
-        if h == 0:
-            out_pass(0)
+
+    product(last, 0, 2)
+    out_last(0)
+    out_pass(0)
+    product(last, 2, 1)
     out_sum_far()
+    product(last, 3, 1)
+    out_last(1)
     for copy in locals_:
         copy.wait_send()
     c.finish()

time: 146 us -> 145 us (level)
  no operation moved by 1% of the time
where the time goes in v1:
time: 145 us
  Pallas kernels  144 us (99%)
    pallas_call x1, Pallas kernels, shards(): pl.pallas_call(kernel, out_shape=pltpu.VMEM((ROWS, WIDTH), BF16), in_spec...  144 us

profile of v1, /device:TPU:0, one launch (start us, length us, event | category | flops | bytes accessed | tf_op | source)
XLA Modules:
  0.0 144.9 jit_solution(7862012375480418836)
XLA Ops:
  0.0 144.2 %swiglu_back.1 = bf16[80,2048]{1,0:T(8,128)(2,1)S(1)} custom-call(bf16[80,2048]{1,0:T(8,128)(2,1)} %x_hbm.1, bf16[80,2048]{1,0:T(8,128)(2,1)} %g_hbm.1, bf16[2048,512]{1,0:T(8,128)(2,1)} %wg_hbm.1, bf16[2048,512]{1,0:T(8,128)(2,1)} %wu_hbm.1, bf16[512,2048]{1,0:T(8,128)(2,1)} %wd_hbm.1), custom_call_target="tpu_custom_call" | custom-call | tf_op jit(solution)/shard_map/swiglu_back/pallas_call | solution.py:498
  144.2 0.7 copy.7

commit v2 on v1

--- a/solution.py
+++ b/solution.py
@@ -93,7 +93,7 @@
 
 OVER_Y = ("ra", "rb", "ga", "gf")
 SENDS = 28
-RECVS = 76
+RECVS = 80
 
 
 def kernel(
@@ -191,10 +191,14 @@
         c.send(f"Az+{dx}", A.at[0, dx], A.at[3, dx], zp)
         c.send(f"Az-{dx}", A.at[0, dx], A.at[1, dx], zm)
 
+    def whole(*names):
+        for name in names:
+            c.need(name)
+            if name + "b" in c.made:
+                c.need(name + "b")
+
     def a_over_z_far(dx):
-        c.need(f"Az+{dx}", f"Az-{dx}")
-        if dx == 0:
-            c.need("Az+0b", "Az-0b")
+        whole(f"Az+{dx}", f"Az-{dx}")
         c.send(f"Azf+{dx}", A.at[3, dx, :, L], A.at[2, dx, :, L], zp, A.at[2, dx])
         c.send(f"Azf-{dx}", A.at[1, dx, :, R], A.at[2, dx, :, R], zm, A.at[2, dx])
 
@@ -203,19 +207,19 @@
         c.send(f"Bx-{dz}", B.at[dz, 0], B.at[dz, 1], xm)
 
     def b_over_x_far(dz):
-        c.need(f"Bx+{dz}", f"Bx-{dz}")
-        if dz == 0:
-            c.need("Bx+0b", "Bx-0b")
+        whole(f"Bx+{dz}", f"Bx-{dz}")
         c.send(f"Bxf+{dz}", B.at[dz, 3, :, L], B.at[dz, 2, :, L], xp, B.at[dz, 2])
         c.send(f"Bxf-{dz}", B.at[dz, 1, :, R], B.at[dz, 2, :, R], xm, B.at[dz, 2])
 
+    def relay_first(piece, rows):
+        c.need(f"Ax+{piece}", f"Ax-{piece}")
+        c.send(f"Az-1{piece}", A.at[0, 1, rows], A.at[1, 1, rows], zm)
+        c.send(f"Az+3{piece}", A.at[0, 3, rows], A.at[3, 3, rows], zp)
+        c.need(f"Bz+{piece}", f"Bz-{piece}")
+        c.send(f"Bx-1{piece}", B.at[1, 0, rows], B.at[1, 1, rows], xm)
+        c.send(f"Bx+3{piece}", B.at[3, 0, rows], B.at[3, 3, rows], xp)
+
     def relay_1():
-        c.need("Ax+", "Ax-", "Ax+b", "Ax-b")
-        c.send("Az-1", A.at[0, 1], A.at[1, 1], zm)
-        c.send("Az+3", A.at[0, 3], A.at[3, 3], zp)
-        c.need("Bz+", "Bz-", "Bz+b", "Bz-b")
-        c.send("Bx-1", B.at[1, 0], B.at[1, 1], xm)
-        c.send("Bx+3", B.at[3, 0], B.at[3, 3], xp)
         c.send("Axf+", A.at[0, 3, :, L], A.at[0, 2, :, L], xp, A.at[0, 2])
         c.send("Axf-", A.at[0, 1, :, R], A.at[0, 2, :, R], xm, A.at[0, 2])
         c.send("Bzf+", B.at[3, 0, :, L], B.at[2, 0, :, L], zp, B.at[2, 0])
@@ -259,13 +263,14 @@
                 if late:
                     c.need(*{0: (), 1: ("Ax-b", "Bx-0b"), 2: (), 3: ("Ax+b", "Bx+0b")}[dx])
                 continue
-            c.need(*{1: (f"Az-{dx}",), 2: (f"Azf+{dx}", f"Azf-{dx}"), 3: (f"Az+{dx}",)}[dz])
+            need = c.need if dx == 0 else whole
+            need(*{1: (f"Az-{dx}",), 2: (f"Azf+{dx}", f"Azf-{dx}"), 3: (f"Az+{dx}",)}[dz])
             if dx == 0:
                 c.need(*{1: ("Bz-",), 2: ("Bzf+", "Bzf-"), 3: ("Bz+",)}[dz])
                 if late:
                     c.need(*{1: ("Az-0b", "Bz-b"), 2: (), 3: ("Az+0b", "Bz+b")}[dz])
             else:
-                c.need(*{1: (f"Bx-{dz}",), 2: (f"Bxf+{dz}", f"Bxf-{dz}"), 3: (f"Bx+{dz}",)}[dx])
+                whole(*{1: (f"Bx-{dz}",), 2: (f"Bxf+{dz}", f"Bxf-{dz}"), 3: (f"Bx+{dz}",)}[dx])
 
     def rows_of(ref, g):
         parts = [ref[dz, dx, first : first + rows] for dz, dx, first, rows in GROUPS[g]]
@@ -284,42 +289,42 @@
             if g == 0:
                 need_weights(q)
             w = Wgu[:, pl.ds(pl.multiple_of(q * 2 * Q, 2 * Q), 2 * Q)]
-            S[g % 2, k, 0:m, 0 : 2 * Q] = jnp.dot(rows_of(A, g), w, preferred_element_type=F32)
+            S[g % 3, k, 0:m, 0 : 2 * Q] = jnp.dot(rows_of(A, g), w, preferred_element_type=F32)
             d = Wd[pl.ds(pl.multiple_of(q * Q, Q), Q), :]
-            S[g % 2, k, 0:m, 2 * Q : 3 * Q] = contract_last(rows_of(B, g), d)
+            S[g % 3, k, 0:m, 2 * Q : 3 * Q] = contract_last(rows_of(B, g), d)
 
     def reduce_far(g):
-        s, m = g % 2, SIZES[g]
+        s, v, m = g % 2, g % 3, SIZES[g]
         at = pl.ds(STARTS[g], m)
         if g >= 2:
             c.free(f"ra+{g - 2}", f"ra-{g - 2}")
-        sa[s, 0:m] = S[s, 0, 0:m].astype(BF16)
+        sa[s, 0:m] = S[v, 0, 0:m].astype(BF16)
         c.send(f"ra+{g}", sa.at[s, pl.ds(0, m), pl.ds(0, CUT)], ra.at[0, at], yp, ra.at[:, at])
         c.send(f"ra-{g}", sa.at[s, pl.ds(0, m), pl.ds(CUT, CUT)], ra.at[1, at], ym, ra.at[:, at])
 
     def reduce_near(g):
-        s, m = g % 2, SIZES[g]
+        s, v, m = g % 2, g % 3, SIZES[g]
         at, rows = slice(STARTS[g], STARTS[g] + m), pl.ds(STARTS[g], m)
         if g >= 2:
             c.free(f"rb+{g - 2}", f"rb-{g - 2}")
         c.need(f"ra+{g}", f"ra-{g}")
-        sb[s, 0, 0:m, 0:CUT] = (S[s, 3, 0:m, 0:CUT] + ra[0, at].astype(F32)).astype(BF16)
-        sb[s, 0, 0:m, CUT:] = S[s, 3, 0:m, CUT:].astype(BF16)
+        sb[s, 0, 0:m, 0:CUT] = (S[v, 3, 0:m, 0:CUT] + ra[0, at].astype(F32)).astype(BF16)
+        sb[s, 0, 0:m, CUT:] = S[v, 3, 0:m, CUT:].astype(BF16)
         c.send(f"rb+{g}", sb.at[s, 0, pl.ds(0, m)], rb.at[0, rows], yp, rb.at[:, rows])
-        sb[s, 1, 0:m, 0:CUT] = S[s, 1, 0:m, 0:CUT].astype(BF16)
-        sb[s, 1, 0:m, CUT:] = (S[s, 1, 0:m, CUT:] + ra[1, at].astype(F32)).astype(BF16)
+        sb[s, 1, 0:m, 0:CUT] = S[v, 1, 0:m, 0:CUT].astype(BF16)
+        sb[s, 1, 0:m, CUT:] = (S[v, 1, 0:m, CUT:] + ra[1, at].astype(F32)).astype(BF16)
         c.send(f"rb-{g}", sb.at[s, 1, pl.ds(0, m)], rb.at[1, rows], ym, rb.at[:, rows])
 
     last = len(GROUPS) - 1
 
     def grads(g):
-        s, m = g % 2, SIZES[g]
+        v, m = g % 3, SIZES[g]
         rows = pl.ds(STARTS[g], m)
         c.need(f"rb+{g}", f"rb-{g}")
 
         def total(at):
             cols = pl.ds(at, Q)
-            return S[s, 2, 0:m, cols] + rb[0, rows, cols].astype(F32) + rb[1, rows, cols].astype(F32)
+            return S[v, 2, 0:m, cols] + rb[0, rows, cols].astype(F32) + rb[1, rows, cols].astype(F32)
 
         gate, upper, hidden_grad = total(0), total(Q), total(2 * Q)
         logistic = 1.0 / (1.0 + jnp.exp(-gate))
@@ -435,27 +440,40 @@
     reduce_far(0)
     forward(0, 1, 4)
     reduce_near(0)
+    relay_first("", ahead)
     forward(1)
     reduce_far(1)
+    relay_first("b", behind)
     relay_1()
     grads(0)
     forward(2)
     reduce_far(2)
     reduce_near(1)
     spread(0)
-    reduce_near(2)
-    grads(1)
     forward(3)
     reduce_far(3)
+    reduce_near(2)
     relay_2()
+    grads(1)
     backward(0)
+    reduce_near(3)
+    relay_3()
+    forward(4)
     spread(1)
-    relay_3()
-    for t in range(3, last):
-        if t > 3:
-            reduce_far(t)
-        if t == 4:
-            relay_4()
+    grads(2)
+    reduce_far(4)
+    relay_4()
+    grads(3)
+    spread(2)
+    backward(1)
+    reduce_near(4)
+    relays[5]()
+    forward(5)
+    spread(3)
+    for t in range(5, last):
+        reduce_far(t)
+        if t == 5:
+            backward(2)
         grads(t - 1)
         backward(t - 2)
         reduce_near(t)
@@ -505,7 +523,7 @@
             pltpu.VMEM((4, 4, ROWS, WIDTH), BF16),
             pltpu.VMEM((WIDTH, 8 * Q), BF16),
             pltpu.VMEM((4 * Q, WIDTH), BF16),
-            pltpu.VMEM((2, 4, TOP, 3 * Q), F32),
+            pltpu.VMEM((3, 4, TOP, 3 * Q), F32),
             pltpu.VMEM((4, 4, ROWS, WIDTH), F32),
             pltpu.VMEM((2, ALL, CUT), BF16),
             pltpu.VMEM((2, ALL, 3 * Q), BF16),
@@ -527,7 +545,7 @@
             pltpu.SemaphoreType.DMA((12,)),
         ],
         compiler_params=pltpu.CompilerParams(
-            collective_id=0, has_side_effects=True, vmem_limit_bytes=65_000_000
+            collective_id=0, has_side_effects=True, vmem_limit_bytes=66_600_000
         ),
         name="swiglu_back",
     )(inputs, out_grad, gate_weight, up_weight, down_weight)

time: 145 us -> 141 us (0.972)
  Pallas kernels: 144 us -> 141 us
    pallas_call x1, Pallas kernels: 144 us -> 141 us  [shards(): pl.pallas_call(kernel, out_shape=pltpu.VMEM((ROWS, WIDTH), BF16), in_spec...]
where the time goes in v2:
time: 141 us
  Pallas kernels  141 us (100%)
    pallas_call x1, Pallas kernels, shards(): pl.pallas_call(kernel, out_shape=pltpu.VMEM((ROWS, WIDTH), BF16), in_spec...  141 us

profile of v2, /device:TPU:0, one launch (start us, length us, event | category | flops | bytes accessed | tf_op | source)
XLA Modules:
  0.0 141.3 jit_solution(9699536314945069052)
XLA Ops:
  0.0 140.6 %swiglu_back.1 = bf16[80,2048]{1,0:T(8,128)(2,1)S(1)} custom-call(bf16[80,2048]{1,0:T(8,128)(2,1)} %x_hbm.1, bf16[80,2048]{1,0:T(8,128)(2,1)} %g_hbm.1, bf16[2048,512]{1,0:T(8,128)(2,1)} %wg_hbm.1, bf16[2048,512]{1,0:T(8,128)(2,1)} %wu_hbm.1, bf16[512,2048]{1,0:T(8,128)(2,1)} %wd_hbm.1), custom_call_target="tpu_custom_call" | custom-call | tf_op jit(solution)/shard_map/swiglu_back/pallas_call | solution.py:516
  140.6 0.7 copy.7

commit v3 on v2

--- a/solution.py
+++ b/solution.py
@@ -15,6 +15,8 @@
 OWN = 512
 Q = 256
 CUT = 3 * Q // 2
+PARTS = 2
+PART = HALF // PARTS
 
 GROUPS = (
     ((0, 0, 0, 80),),
@@ -93,7 +95,7 @@
 
 OVER_Y = ("ra", "rb", "ga", "gf")
 SENDS = 28
-RECVS = 80
+RECVS = 86
 
 
 def kernel(
@@ -359,8 +361,13 @@
                 O[dz, dx, first : first + count, cols] = o[done : done + count]
                 done += count
 
-    def backward(g):
-        product(g)
+    def backward(g, between=None):
+        if between is None:
+            product(g)
+        else:
+            product(g, 0, 2)
+            reduce_near(between)
+            product(g, 2, 2)
         run(after.get(g, ()))
 
     def out_down(r):
@@ -373,13 +380,18 @@
             c.need("d1", "d3")
             total = total + xd[1].astype(F32) + xd[3].astype(F32)
         xsa[r] = total.astype(BF16)
-        c.send(f"xa+{r}", xsa.at[r, :, L], xa.at[r // 2, 0], xp, xa.at[r // 2])
-        c.send(f"xa-{r}", xsa.at[r, :, R], xa.at[r // 2, 1], xm, xa.at[r // 2])
-
-    def out_pass(r):
-        c.need(f"xa+{r}", f"xa-{r}")
-        c.send(f"xd+{r}", xa.at[r // 2, 0], xd.at[r, :, L], xp, xd.at[r])
-        c.send(f"xd-{r}", xa.at[r // 2, 1], xd.at[r, :, R], xm, xd.at[r])
+        for p in range(PARTS):
+            here, there = pl.ds(p * PART, PART), pl.ds(HALF + p * PART, PART)
+            both = xa.at[r // 2, :, :, here]
+            c.send(f"xa+{r}_{p}", xsa.at[r, :, here], xa.at[r // 2, 0, :, here], xp, both)
+            c.send(f"xa-{r}_{p}", xsa.at[r, :, there], xa.at[r // 2, 1, :, here], xm, both)
+
+    def out_pass(r, p):
+        here, there = pl.ds(p * PART, PART), pl.ds(HALF + p * PART, PART)
+        both = xd.at[r, :, pl.ds(0, 2 * PART)]
+        c.need(f"xa+{r}_{p}", f"xa-{r}_{p}")
+        c.send(f"xd+{r}_{p}", xa.at[r // 2, 0, :, here], xd.at[r, :, here], xp, both)
+        c.send(f"xd-{r}_{p}", xa.at[r // 2, 1, :, here], xd.at[r, :, there], xm, both)
 
     def out_near(r, dx, rows=(0, ROWS), halves=(0, 1)):
         k, sign, device = {1: (0, "+", xp), 3: (1, "-", xm)}[dx]
@@ -395,21 +407,26 @@
     def out_sum(r, rows=(0, ROWS), halves=(0, 1)):
         c.need(f"xb+{r}_0_0", f"xb-{r}_0_0")
         if r == 2:
-            c.need("xd+2", "xd-2")
+            c.need(*(f"xd+2_{p}" for p in range(PARTS)))
         at, to = slice(*rows), pl.ds(rows[0], rows[1] - rows[0])
         cols = pl.ds(halves[0] * HALF, len(halves) * HALF)
         zs[r - 1, at, cols] = over_x(r, at, cols).astype(BF16)
         if r == 2:
-            c.send("z2+", zs.at[1, :, L], zt.at[0], zp, zt)
-            c.send("z2-", zs.at[1, :, R], zt.at[1], zm, zt)
+            for p in range(PARTS):
+                here, there = pl.ds(p * PART, PART), pl.ds(HALF + p * PART, PART)
+                both = zt.at[:, :, here]
+                c.send(f"z2+{p}", zs.at[1, :, here], zt.at[0, :, here], zp, both)
+                c.send(f"z2-{p}", zs.at[1, :, there], zt.at[1, :, here], zm, both)
         else:
             name = f"z{r}_{rows[0]}_{halves[0]}"
             c.send(name, zs.at[r - 1, to, cols], zr.at[r - 1, to, cols], {1: zp, 3: zm}[r])
 
-    def out_sum_far():
-        c.need("z2+", "z2-")
-        c.send("z2f+", zt.at[0], zr.at[1, :, L], zp, zr.at[1])
-        c.send("z2f-", zt.at[1], zr.at[1, :, R], zm, zr.at[1])
+    def out_sum_far(p):
+        here, there = pl.ds(p * PART, PART), pl.ds(HALF + p * PART, PART)
+        both = zr.at[1, :, pl.ds(0, 2 * PART)]
+        c.need(f"z2+{p}", f"z2-{p}")
+        c.send(f"z2f+{p}", zt.at[0, :, here], zr.at[1, :, here], zp, both)
+        c.send(f"z2f-{p}", zt.at[1, :, here], zr.at[1, :, there], zm, both)
 
     def out_final(first, rows):
         at = slice(first, first + rows)
@@ -475,17 +492,16 @@
         if t == 5:
             backward(2)
         grads(t - 1)
-        backward(t - 2)
-        reduce_near(t)
+        backward(t - 2, t)
         if t + 1 in relays:
             relays[t + 1]()
         forward(t + 1)
         spread(t - 1)
     reduce_far(last)
     grads(last - 1)
-    out_pass(2)
-    backward(last - 2)
-    reduce_near(last)
+    for p in range(PARTS):
+        out_pass(2, p)
+    backward(last - 2, last)
     spread(last - 1)
     grads(last)
     backward(last - 1)
@@ -498,12 +514,14 @@
         out_sum(1, (EARLY, ROWS), (h,))
         out_sum(3, (EARLY, ROWS), (h,))
 
-    product(last, 0, 2)
+    product(last, 0, 1)
+    out_pass(0, 0)
+    out_sum_far(0)
+    product(last, 1, 1)
     out_last(0)
-    out_pass(0)
-    product(last, 2, 1)
-    out_sum_far()
-    product(last, 3, 1)
+    out_pass(0, 1)
+    out_sum_far(1)
+    product(last, 2, 2)
     out_last(1)
     for copy in locals_:
         copy.wait_send()

time: 141 us -> 140 us (level)
  Pallas kernels: 141 us -> 139 us
where the time goes in v3:
time: 140 us
  Pallas kernels  139 us (99%)
    pallas_call x1, Pallas kernels, shards(): pl.pallas_call(kernel, out_shape=pltpu.VMEM((ROWS, WIDTH), BF16), in_spec...  139 us

profile of v3, /device:TPU:0, one launch (start us, length us, event | category | flops | bytes accessed | tf_op | source)
XLA Modules:
  0.0 140.0 jit_solution(17994169783497956000)
XLA Ops:
  0.0 139.3 %swiglu_back.1 = bf16[80,2048]{1,0:T(8,128)(2,1)S(1)} custom-call(bf16[80,2048]{1,0:T(8,128)(2,1)} %x_hbm.1, bf16[80,2048]{1,0:T(8,128)(2,1)} %g_hbm.1, bf16[2048,512]{1,0:T(8,128)(2,1)} %wg_hbm.1, bf16[2048,512]{1,0:T(8,128)(2,1)} %wu_hbm.1, bf16[512,2048]{1,0:T(8,128)(2,1)} %wd_hbm.1), custom_call_target="tpu_custom_call" | custom-call | tf_op jit(solution)/shard_map/swiglu_back/pallas_call | solution.py:534
  139.3 0.7 copy.7

commit v4 on v3

--- a/solution.py
+++ b/solution.py
@@ -94,7 +94,7 @@
 
 
 OVER_Y = ("ra", "rb", "ga", "gf")
-SENDS = 28
+SENDS = 24
 RECVS = 86
 
 
@@ -162,7 +162,7 @@
                 src_ref=src,
                 dst_ref=dst,
                 send_sem=weight_sends.at[3 * n + k],
-                recv_sem=weight_sems.at[3 * q + k],
+                recv_sem=weight_sems.at[2 * q + k // 2],
                 device_id=partner,
                 device_id_type=MESH,
             )
@@ -186,8 +186,10 @@
     own_over_z("Bz@b", g_hbm, B, behind)
 
     def need_weights(q):
-        for k, (src, dst) in enumerate(pieces(q, 0)):
-            pltpu.make_async_copy(src, dst, weight_sems.at[3 * q + k]).wait()
+        wide = Wgu.at[:, pl.ds(pl.multiple_of(q * 2 * Q, 2 * Q), 2 * Q)]
+        narrow = Wd.at[pl.ds(pl.multiple_of(q * Q, Q), Q)]
+        for k, ref in enumerate((wide, narrow)):
+            pltpu.make_async_copy(ref, ref, weight_sems.at[2 * q + k]).wait()
 
     def a_over_z(dx):
         c.send(f"Az+{dx}", A.at[0, dx], A.at[3, dx], zp)
@@ -441,7 +443,6 @@
         4: ((out_near, 1, 3), (out_near, 3, 1)),
         5: ((out_far, 2), (out_down, 1), (out_sum, 1, (0, EARLY)), (out_sum, 3, (0, EARLY))),
         6: ((out_down, 3), (out_near, 2, 1), (out_near, 2, 3)),
-        7: ((out_far, 0),),
     }
 
     def run(events):
@@ -450,7 +451,7 @@
 
     for n, (q, j) in enumerate(own):
         for k, (src, dst) in enumerate(pieces(q, j)):
-            local(src, dst, weight_sems.at[3 * q + k])
+            local(src, dst, weight_sems.at[2 * q + k // 2])
     for copy in own_tokens:
         copy.wait()
     forward(0, 0, 1)
@@ -506,6 +507,7 @@
     grads(last)
     backward(last - 1)
     spread(last)
+    out_far(0)
     out_sum(2)
 
     def out_last(h):
@@ -560,7 +562,7 @@
             pltpu.SemaphoreType.DMA((RECVS,)),
             pltpu.SemaphoreType.DMA((2,)),
             pltpu.SemaphoreType.DMA((6,)),
-            pltpu.SemaphoreType.DMA((12,)),
+            pltpu.SemaphoreType.DMA((8,)),
         ],
         compiler_params=pltpu.CompilerParams(
             collective_id=0, has_side_effects=True, vmem_limit_bytes=66_600_000

time: 140 us -> 140 us (level)
  no operation moved by 1% of the time
where the time goes in v4:
time: 140 us
  Pallas kernels  139 us (99%)
    pallas_call x1, Pallas kernels, shards(): pl.pallas_call(kernel, out_shape=pltpu.VMEM((ROWS, WIDTH), BF16), in_spec...  139 us

profile of v4, /device:TPU:0, one launch (start us, length us, event | category | flops | bytes accessed | tf_op | source)
XLA Modules:
  0.0 139.7 jit_solution(15056228614890090809)
XLA Ops:
  0.0 139.0 %swiglu_back.1 = bf16[80,2048]{1,0:T(8,128)(2,1)S(1)} custom-call(bf16[80,2048]{1,0:T(8,128)(2,1)} %x_hbm.1, bf16[80,2048]{1,0:T(8,128)(2,1)} %g_hbm.1, bf16[2048,512]{1,0:T(8,128)(2,1)} %wg_hbm.1, bf16[2048,512]{1,0:T(8,128)(2,1)} %wu_hbm.1, bf16[512,2048]{1,0:T(8,128)(2,1)} %wd_hbm.1), custom_call_target="tpu_custom_call" | custom-call | tf_op jit(solution)/shard_map/swiglu_back/pallas_call | solution.py:536
  139.0 0.7 copy.7
